TPU v7x, 32 devices: a whole 2x2x4 slice. The times are simulated.
32 devices in a mesh: dp: 2 (over x), expert: 16 (over z, y, core).
Axes of the slice: x: 2, y: 2, z: 4, core: 2. Of those that a mesh axis runs over, the one named last changes fastest.
Arguments:
- queries: bfloat16 [1024, 4, 3072], P('expert', 'dp'), may hold values from -256 to 256
- key_nope: bfloat16 [1024, 4, 2048], P('expert', 'dp'), may hold values from -4 to 4
- key_rope: bfloat16 [1024, 4, 64], P('expert', 'dp'), may hold values from -4 to 4
- values: bfloat16 [1024, 4, 2048], P('expert', 'dp'), may hold values from -6 to 6
- residual: bfloat16 [1024, 4, 2048], P('expert', 'dp'), may hold values from -6 to 6
- segments: int32 [4, 1024], P('dp'), may hold values from 0 to 1, never falling along the last dimension, each value on 1 to 768 neighbouring positions
- out_proj: bfloat16 [2048, 2048], P(('dp', 'expert')), may hold values from -0.125 to 0.125
- norm_gain: bfloat16 [2048], replicated, may hold values from 0.5 to 1.5
- expert_gate: bfloat16 [16, 2048, 704], P('expert'), may hold values from -0.125 to 0.125
- expert_up: bfloat16 [16, 2048, 704], P('expert'), may hold values from -0.125 to 0.125
- expert_down: bfloat16 [16, 704, 2048], P('expert'), may hold values from -0.21875 to 0.21875
- routes: int32 [2, 16, 128, 6], P('dp', 'expert'), may hold values from 0 to 15, all different within a row; in each aligned block of 128 rows (0 to 127, 128 to 255, ..., all dimensions but the last counted through in order) at most 72 rows name the same one
- route_weights: float32 [2, 16, 128, 6], P('dp', 'expert'), may hold values from 0.1 to 0.6
Outputs:
- layer_out: bfloat16 [1024, 4, 2048], P('expert', 'dp')
Inputs may be any that keep to these rules, and one draw needn't show every extreme that they name: `routes`: each row names 6 different experts; within the rows of one device no expert is named more than 72 times.
All inputs are finite; a program needn't handle non-finite values.
Results may differ from a plain program's by a relative error of at most 0.0049.
Values may be sent and summed in bfloat16 or wider, within the bound.
A program may use at most 128 MiB of HBM per device.

v0:
```python
import jax
import jax.numpy as jnp
from jax import lax
from jax.sharding import PartitionSpec as P

HEADS = 16
NOPE = 128
ROPE = 64
V_DIM = 128
TOP = 6


EPSILON = 1e-06
QUERY_BLOCK = 512


def feed_forward(rows, gate_matrix, up_matrix, down_matrix):
    gate_part = jnp.dot(rows, gate_matrix, preferred_element_type=jnp.float32)
    up_part = jnp.dot(rows, up_matrix, preferred_element_type=jnp.float32)
    activated = (jax.nn.silu(gate_part) * up_part).astype(jnp.bfloat16)
    return jnp.dot(activated, down_matrix, preferred_element_type=jnp.float32).astype(jnp.bfloat16)


def attend_items(query_items, key_items, value_items, segment_items):
    length, count_items, qk_width = query_items.shape
    block_rows = QUERY_BLOCK
    score_scale = qk_width ** (-0.5)
    key_positions = jnp.arange(length, dtype=jnp.int32)

    def one_block(block_index):
        first_row = block_index * block_rows
        query_block = lax.dynamic_slice_in_dim(query_items, first_row, block_rows, 0)
        scores = (
            jnp.einsum("qid,kid->iqk", query_block, key_items, preferred_element_type=jnp.float32)
            * score_scale
        )
        row_positions = first_row + jnp.arange(block_rows, dtype=jnp.int32)
        row_segments = lax.dynamic_slice_in_dim(segment_items, first_row, block_rows, 1)
        allowed = (row_positions[None, :, None] >= key_positions[None, None, :]) & (
            row_segments[:, :, None] == segment_items[:, None, :]
        )
        scores = jnp.where(allowed, scores, -jnp.inf)
        row_peak = jnp.max(scores, axis=2, keepdims=True)
        raised = jnp.exp(scores - row_peak)
        weights = (raised / jnp.sum(raised, axis=2, keepdims=True)).astype(jnp.bfloat16)
        return jnp.einsum(
            "iqk,kid->qid", weights, value_items, preferred_element_type=jnp.float32
        ).astype(jnp.bfloat16)

    blocks = lax.map(one_block, jnp.arange(length // block_rows, dtype=jnp.int32))
    return blocks.reshape(length, count_items, value_items.shape[2])


def body(
    queries,
    key_nope,
    key_rope,
    values,
    residual,
    segments,
    out_proj,
    norm_gain,
    expert_gate,
    expert_up,
    expert_down,
    routes,
    route_weights,
):
    half_rows, stream_count, query_width = queries.shape
    model_width = residual.shape[2]
    token_rows = half_rows * stream_count
    pair_count = token_rows * TOP
    expert_count = lax.axis_size("expert")
    item_count = stream_count * HEADS // expert_count
    key_heads = jnp.concatenate(
        [
            key_nope.reshape(half_rows, stream_count, HEADS, NOPE),
            jnp.broadcast_to(key_rope[:, :, None, :], (half_rows, stream_count, HEADS, ROPE)),
        ],
        axis=3,
    )
    query_items = queries.reshape(half_rows, stream_count * HEADS, NOPE + ROPE)
    key_items = key_heads.reshape(half_rows, stream_count * HEADS, NOPE + ROPE)
    value_items = values.reshape(half_rows, stream_count * HEADS, V_DIM)
    query_all, key_all, value_all = (
        lax.all_to_all(query_items, "expert", split_axis=1, concat_axis=0, tiled=True),
        lax.all_to_all(key_items, "expert", split_axis=1, concat_axis=0, tiled=True),
        lax.all_to_all(value_items, "expert", split_axis=1, concat_axis=0, tiled=True),
    )
    item_ids = lax.axis_index("expert") * item_count + jnp.arange(item_count, dtype=jnp.int32)
    stream_ids = item_ids // HEADS
    selector = (stream_ids[:, None] == jnp.arange(stream_count, dtype=jnp.int32)[None, :]).astype(
        jnp.int32
    )
    segment_items = jnp.sum(selector[:, :, None] * segments[None, :, :], axis=1)
    attended_items = attend_items(query_all, key_all, value_all, segment_items)
    attended_back = lax.all_to_all(
        attended_items, "expert", split_axis=0, concat_axis=1, tiled=True
    )
    attn_rows = attended_back.reshape(token_rows, HEADS * V_DIM)
    projected = jnp.dot(
        attn_rows,
        lax.all_gather(out_proj, ("dp", "expert"), axis=0, tiled=True),
        preferred_element_type=jnp.float32,
    )
    hidden = residual.reshape(token_rows, model_width).astype(jnp.float32) + projected
    mean_square = jnp.mean(hidden * hidden, axis=1, keepdims=True)
    normed = (hidden * lax.rsqrt(mean_square + EPSILON) * norm_gain.astype(jnp.float32)).astype(
        jnp.bfloat16
    )
    capacity = min(token_rows, max(2, token_rows * TOP * 3 // (2 * expert_count)))
    flat_routes = routes.reshape(pair_count)
    matches = (flat_routes[:, None] == jnp.arange(expert_count, dtype=jnp.int32)[None, :]).astype(
        jnp.int32
    )
    earlier = jnp.cumsum(matches, axis=0) - matches
    slot_rank = jnp.sum(earlier * matches, axis=1)
    target = flat_routes * capacity + slot_rank
    pair_ids = jnp.arange(pair_count, dtype=jnp.int32)
    slot_source = (
        jnp.full((expert_count * capacity,), pair_count, jnp.int32).at[target].set(pair_ids)
    )
    slot_live = slot_source < pair_count
    slot_rows = normed[jnp.minimum(slot_source, pair_count - 1) // TOP]
    outgoing = jnp.where(slot_live[:, None], slot_rows, jnp.zeros_like(slot_rows)).reshape(
        expert_count, capacity, model_width
    )
    gate_matrix = expert_gate[0]
    up_matrix = expert_up[0]
    down_matrix = expert_down[0]
    arrived = lax.all_to_all(outgoing, "expert", split_axis=0, concat_axis=0, tiled=True)
    source_count, slot_count, width = arrived.shape
    flat_rows = arrived.reshape(source_count * slot_count, width)
    results = feed_forward(flat_rows, gate_matrix, up_matrix, down_matrix)
    returned = lax.all_to_all(
        results.reshape(source_count, slot_count, width),
        "expert",
        split_axis=0,
        concat_axis=0,
        tiled=True,
    )
    pair_outputs = returned.reshape(expert_count * capacity, model_width)[target]
    weighted = route_weights.reshape(pair_count, 1) * pair_outputs.astype(jnp.float32)
    routed_sum = jnp.sum(weighted.reshape(token_rows, TOP, model_width), axis=1)
    layer_out = (hidden + routed_sum).astype(jnp.bfloat16)
    return layer_out.reshape(half_rows, stream_count, model_width)


def solution(mesh):
    return jax.shard_map(
        body,
        mesh=mesh,
        in_specs=(
            P("expert", "dp", None),
            P("expert", "dp", None),
            P("expert", "dp", None),
            P("expert", "dp", None),
            P("expert", "dp", None),
            P("dp", None),
            P(("dp", "expert"), None),
            P(),
            P("expert", None, None),
            P("expert", None, None),
            P("expert", None, None),
            P("dp", "expert", None, None),
            P("dp", "expert", None, None),
        ),
        out_specs=P("expert", "dp", None),
        check_vma=False,
    )
```

profile of v0, /device:TPU:15, one launch (start us, length us, event | category | flops | bytes accessed | tf_op | source)
XLA Modules:
  0.0 449.9 jit_solution(12819666800241696659)
XLA Ops:
  9.8 6.5 %all-to-all-start.2 = ((bf16[64,32,128]{2,0,1:T(8,128)(2,1)}), bf16[64,32,128]{2,0,1:T(8,128)(2,1)S(1)}, u32[]{:S(2)}, u32[]{:S(2)}) async-start(bf16[64,32,128]{2,0,1:T(8,128)(2,1)} %copy.62), calls=%async_computation.2 | async-start | bytes 1048576 | tf_op jit(solution)/shard_map/all_to_all | solution.py:88
  21.5 14.1 %all-to-all-done.2 = bf16[64,32,128]{2,0,1:T(8,128)(2,1)S(1)} async-done(((bf16[64,32,128]{2,0,1:T(8,128)(2,1)}), bf16[64,32,128]{2,0,1:T(8,128)(2,1)S(1)}, u32[]{:S(2)}, u32[]{:S(2)}) %all-to-all-start.2) | async-done | bytes 524320 | tf_op jit(solution)/shard_map/all_to_all | solution.py:88
  35.6 4.9 %all-to-all-start.1 = ((bf16[64,32,192]{2,0,1:T(8,128)(2,1)}), bf16[64,32,192]{2,0,1:T(8,128)(2,1)}, u32[]{:S(2)}, u32[]{:S(2)}) async-start(bf16[64,32,192]{2,0,1:T(8,128)(2,1)} %copy.60), calls=%async_computation.1 | async-start | bytes 2097152 | tf_op jit(solution)/shard_map/all_to_all | solution.py:87
  46.7 29.9 %all-to-all-done.1 = bf16[64,32,192]{2,0,1:T(8,128)(2,1)} async-done(((bf16[64,32,192]{2,0,1:T(8,128)(2,1)}), bf16[64,32,192]{2,0,1:T(8,128)(2,1)}, u32[]{:S(2)}, u32[]{:S(2)}) %all-to-all-start.1) | async-done | bytes 786464 | tf_op jit(solution)/shard_map/all_to_all | solution.py:87
  76.6 5.1 %all-to-all-start = ((bf16[64,32,192]{2,0,1:T(8,128)(2,1)}), bf16[64,32,192]{2,0,1:T(8,128)(2,1)}, u32[]{:S(2)}, u32[]{:S(2)}) async-start(bf16[64,32,192]{2,0,1:T(8,128)(2,1)} %copy.58), calls=%async_computation | async-start | bytes 2097152 | tf_op jit(solution)/shard_map/all_to_all | solution.py:86
  89.7 34.7 %all-to-all-done = bf16[64,32,192]{2,0,1:T(8,128)(2,1)} async-done(((bf16[64,32,192]{2,0,1:T(8,128)(2,1)}), bf16[64,32,192]{2,0,1:T(8,128)(2,1)}, u32[]{:S(2)}, u32[]{:S(2)}) %all-to-all-start) | async-done | bytes 786464 | tf_op jit(solution)/shard_map/all_to_all | solution.py:86
  129.0 20.0 %while.11 = (s32[]{:T(128)}, bf16[2,512,2,128]{3,1,0,2:T(8,128)(2,1)}, s32[2]{0:T(128)S(1)}, s32[2,1024]{1,0:T(2,128)S(1)}, bf16[1024,2,192]{0,2,1:T(8,128)(2,1)...) while((s32[]{:T(128)}, ...), condition=%wide.region_4.5_spmd.clone, body=%wide.region_1.4_spmd.clone.sunk | while | flops 1088032256 | bytes 4764343 | solution.py:50
  130.7 3.4 fusion.73
  134.1 4.9 %fusion.74 = bf16[2,512,2,128]{3,1,0,2:T(8,128)(2,1)} fusion(bf16[2,512,2,128]{3,1,0,2:T(8,128)(2,1)} %get-tuple-element.163, s32[]{:T(128)} %get-tuple-element.162, bf16[1024,2,128]{2,0,1:T(8,128)(2,1)} %get-tuple-element.179, f32[2,512]{1,0:T(2,128)S(1)} %fusion.73, s32[2,1024]{1,0:T(2,128)S(1)} %get-tuple-element.176, ...), kind=kOutput, calls=%fused_computation.18.clone.1 | convolution fusion | flops 678561792 | bytes 2507268 | tf_op jit(solution)/shard_map/while/body/eval_jaxpr/iqk,kid->qid/dot_general | solution.py:46
  144.1 5.0 %fusion.74 = bf16[2,512,2,128]{3,1,0,2:T(8,128)(2,1)} fusion(bf16[2,512,2,128]{3,1,0,2:T(8,128)(2,1)} %get-tuple-element.163, s32[]{:T(128)} %get-tuple-element.162, bf16[1024,2,128]{2,0,1:T(8,128)(2,1)} %get-tuple-element.179, f32[2,512]{1,0:T(2,128)S(1)} %fusion.73, s32[2,1024]{1,0:T(2,128)S(1)} %get-tuple-element.176, ...), kind=kOutput, calls=%fused_computation.18.clone.1 | convolution fusion | flops 678561792 | bytes 2507268 | tf_op jit(solution)/shard_map/while/body/eval_jaxpr/iqk,kid->qid/dot_general | solution.py:46
  151.4 4.9 %all-to-all-start.3 = ((bf16[1024,2,128]{2,1,0:T(2,128)(2,1)}), bf16[1024,2,128]{2,1,0:T(2,128)(2,1)S(1)}, u32[]{:S(2)}, u32[]{:S(2)}) async-start(bf16[1024,2,128]{2,1,0:T(2,128)(2,1)} %copy.67), calls=%async_computation.3 | async-start | bytes 1048576 | tf_op jit(solution)/shard_map/all_to_all | solution.py:97
  159.0 3.6 scatter_custom_fusion
  162.8 7.2 %all-to-all-done.3 = bf16[1024,2,128]{2,1,0:T(2,128)(2,1)S(1)} async-done(((bf16[1024,2,128]{2,1,0:T(2,128)(2,1)}), bf16[1024,2,128]{2,1,0:T(2,128)(2,1)S(1)}, u32[]{:S(2)}, u32[]{:S(2)}) %all-to-all-start.3) | async-done | bytes 524320 | tf_op jit(solution)/shard_map/all_to_all | solution.py:97
  172.5 5.0 %multiply_reduce_fusion.1 = (f32[128]{0:T(128)S(1)}, f32[128,2048]{1,0:T(8,128)S(1)}) fusion(f32[128,2048]{1,0:T(8,128)} %reshape.201, bf16[128,2048]{1,0:T(8,128)(2,1)S(1)} %reshape.195, bf16[2048,2048]{1,0:T(8,128)(2,1)} %all-gather.2.cloned.1.call-done), kind=kOutput, calls=%fused_computation.45 | convolution fusion | flops 1074528128 | bytes 11010560 | tf_op jit(solution)/shard_map/dot_general | solution.py:101
  178.7 5.9 %gather_fusion = bf16[1152,2048]{1,0:T(8,128)(2,1)} fusion(bf16[128,2048]{1,0:T(8,128)(2,1)S(1)} %multiply_convert_fusion, s32[2048]{0:T(1024)S(1)} %pad_clamp_fusion), kind=kCustom, calls=%fused_computation | custom fusion | bytes 9441792 | tf_op jit(solution)/shard_map/gather | solution.py:124
  187.4 108.4 %all_to_all.79 = bf16[16,72,2048]{2,1,0:T(8,128)(2,1)S(1)} all-to-all(bf16[16,72,2048]{2,1,0:T(8,128)(2,1)S(1)} %broadcast_select_fusion), channel_id=1, replica_groups=mesh['dp'=2,'expert'=16] {'expert'}, dimensions={0} | all-to-all | bytes 9437184 | tf_op jit(solution)/shard_map/all_to_all | solution.py:131
  295.7 4.0 fusion.40
  299.8 4.0 fusion.37
  303.8 5.6 %convolution_convert_fusion = bf16[1152,2048]{1,0:T(8,128)(2,1)} fusion(bf16[1152,704]{0,1:T(8,128)(2,1)S(1)} %fusion.37, bf16[1,704,2048]{2,1,0:T(8,128)(2,1)S(1)} %copy-done), kind=kOutput, calls=%fused_computation.33 | convolution fusion | flops 3324248064 | bytes 9224192 | tf_op jit(solution)/shard_map/dot_general | solution.py:21
  309.4 5.4 %all-to-all-start.5 = ((bf16[16,72,2048]{2,1,0:T(8,128)(2,1)}), bf16[16,72,2048]{2,1,0:T(8,128)(2,1)}, u32[]{:S(2)}, u32[]{:S(2)}) async-start(bf16[16,72,2048]{2,1,0:T(8,128)(2,1)} %bitcast.86), calls=%async_computation.5 | async-start | bytes 9437184 | tf_op jit(solution)/shard_map/all_to_all | solution.py:135
  314.9 103.6 %all-to-all-done.5 = bf16[16,72,2048]{2,1,0:T(8,128)(2,1)} async-done(((bf16[16,72,2048]{2,1,0:T(8,128)(2,1)}), bf16[16,72,2048]{2,1,0:T(8,128)(2,1)}, u32[]{:S(2)}, u32[]{:S(2)}) %all-to-all-start.5) | async-done | bytes 4718624 | tf_op jit(solution)/shard_map/all_to_all | solution.py:135
  418.5 10.0 %gather_fusion.1 = bf16[768,2048]{1,0:T(8,128)(2,1)} fusion(bf16[1152,2048]{1,0:T(8,128)(2,1)} %bitcast.21, s32[1024]{0:T(1024)S(1)} %pad_clamp_fusion.1), kind=kCustom, calls=%fused_computation.1 | custom fusion | bytes 6294528 | tf_op jit(solution)/shard_map/gather | solution.py:142
  428.5 6.6 %reshape.202 = f32[128,6,2048]{2,1,0:T(8,128)} reshape(bf16[768,2048]{1,0:T(8,128)(2,1)} %gather_fusion.1) | data formatting | bytes 9437184 | tf_op jit(solution)/shard_map/convert_element_type | solution.py:143
  435.1 6.7 %multiply_reduce_fusion = f32[128,2048]{1,0:T(8,128)S(1)} fusion(f32[128,6,2048]{2,1,0:T(8,128)} %reshape.202, f32[128,6]{1,0:T(8,128)S(1)} %bitcast.97), kind=kLoop, calls=%fused_computation.32 | loop fusion | flops 2883584 | bytes 7343104 | tf_op jit(solution)/shard_map/reduce_sum | solution.py:144
  (79 shorter events, 45.6 us)
Async XLA Ops:
  6.5 297.2 %copy-start = (bf16[1,704,2048]{2,1,0:T(8,128)(2,1)S(1)}, bf16[1,704,2048]{2,1,0:T(8,128)(2,1)}, u32[]{:S(2)}) copy-start(bf16[1,704,2048]{2,1,0:T(8,128)(2,1)} %param.25) | copy-start | bytes 8650756
  6.5 12.0 %copy-start.3 = (bf16[64,2,64]{2,1,0:T(2,128)(2,1)S(1)}, bf16[64,2,64]{2,1,0:T(2,128)(2,1)}, u32[]{:S(2)}) copy-start(bf16[64,2,64]{2,1,0:T(2,128)(2,1)} %param.17) | copy-start | bytes 49156
  6.5 166.0 %all-gather.2.cloned.1.call-start = ((), (), s32[]{:S(2)}) async-start(), calls=%async_computation.6 | async-start | bytes 8650752 | tf_op jit(solution)/shard_map/all_gather | solution.py:103
  9.8 25.8 %all-to-all-start.2 = ((bf16[64,32,128]{2,0,1:T(8,128)(2,1)}), bf16[64,32,128]{2,0,1:T(8,128)(2,1)S(1)}, u32[]{:S(2)}, u32[]{:S(2)}) async-start(bf16[64,32,128]{2,0,1:T(8,128)(2,1)} %copy.62), calls=%async_computation.2 | async-start | bytes 1048576 | tf_op jit(solution)/shard_map/all_to_all | solution.py:88
  21.5 60.2 %copy-start.4 = (s32[1,1,128,6]{2,1,3,0:T(1,128)S(1)}, s32[1,1,128,6]{2,1,3,0:T(1,128)}, u32[]{:S(2)}) copy-start(s32[1,1,128,6]{2,1,3,0:T(1,128)} %param.26) | copy-start | bytes 9220
  21.5 62.7 %copy-start.5 = (s32[2,1024]{1,0:T(2,128)S(1)}, s32[2,1024]{1,0:T(2,128)}, u32[]{:S(2)}) copy-start(s32[2,1024]{1,0:T(2,128)} %param.20) | copy-start | bytes 24580
  35.6 41.0 %all-to-all-start.1 = ((bf16[64,32,192]{2,0,1:T(8,128)(2,1)}), bf16[64,32,192]{2,0,1:T(8,128)(2,1)}, u32[]{:S(2)}, u32[]{:S(2)}) async-start(bf16[64,32,192]{2,0,1:T(8,128)(2,1)} %copy.60), calls=%async_computation.1 | async-start | bytes 2097152 | tf_op jit(solution)/shard_map/all_to_all | solution.py:87
  76.6 47.8 %all-to-all-start = ((bf16[64,32,192]{2,0,1:T(8,128)(2,1)}), bf16[64,32,192]{2,0,1:T(8,128)(2,1)}, u32[]{:S(2)}, u32[]{:S(2)}) async-start(bf16[64,32,192]{2,0,1:T(8,128)(2,1)} %copy.58), calls=%async_computation | async-start | bytes 2097152 | tf_op jit(solution)/shard_map/all_to_all | solution.py:86
  129.0 29.9 %copy-start.6 = (bf16[2048]{0:T(1024)(128)(2,1)S(1)}, bf16[2048]{0:T(1024)(128)(2,1)}, u32[]{:S(2)}) copy-start(bf16[2048]{0:T(1024)(128)(2,1)} %param.22) | copy-start | bytes 12292
  151.4 18.5 %all-to-all-start.3 = ((bf16[1024,2,128]{2,1,0:T(2,128)(2,1)}), bf16[1024,2,128]{2,1,0:T(2,128)(2,1)S(1)}, u32[]{:S(2)}, u32[]{:S(2)}) async-start(bf16[1024,2,128]{2,1,0:T(2,128)(2,1)} %copy.67), calls=%async_computation.3 | async-start | bytes 1048576 | tf_op jit(solution)/shard_map/all_to_all | solution.py:97
  177.5 1.0 copy-start.1
  187.3 108.4 %copy-start.8 = (bf16[1,2048,704]{1,2,0:T(8,128)(2,1)S(1)}, bf16[1,2048,704]{1,2,0:T(8,128)(2,1)}, u32[]{:S(2)}) copy-start(bf16[1,2048,704]{1,2,0:T(8,128)(2,1)} %param.23) | copy-start | bytes 8650756
  295.7 4.0 copy-start.9
  309.4 5.4 %copy-start.7 = (f32[1,1,128,6]{2,1,3,0:T(1,128)S(1)}, f32[1,1,128,6]{2,1,3,0:T(1,128)}, u32[]{:S(2)}) copy-start(f32[1,1,128,6]{2,1,3,0:T(1,128)} %param.27) | copy-start | bytes 9220
  309.4 109.1 %all-to-all-start.5 = ((bf16[16,72,2048]{2,1,0:T(8,128)(2,1)}), bf16[16,72,2048]{2,1,0:T(8,128)(2,1)}, u32[]{:S(2)}, u32[]{:S(2)}) async-start(bf16[16,72,2048]{2,1,0:T(8,128)(2,1)} %bitcast.86), calls=%async_computation.5 | async-start | bytes 9437184 | tf_op jit(solution)/shard_map/all_to_all | solution.py:135
  435.1 6.7 %copy-start.2 = (f32[128,2048]{1,0:T(8,128)S(1)}, f32[128,2048]{1,0:T(8,128)}, u32[]{:S(2)}) copy-start(f32[128,2048]{1,0:T(8,128)} %copy-done.1) | copy-start | bytes 3145732
Sparse Core Ops, SparseCore 0:
  10.2 110.8 all-gather.1
where the time goes:
time: 451 us; the launch traced here: 450 us
  waiting for transfers between devices  190 us (42%)
  blocking collectives  108 us (24%)
  local copies, waits for them, and re-layouts  60.4 us (13%)
  matrix products  35.2 us (8%)
  starting transfers between devices  26.8 us (6%)
  other arithmetic  13.9 us (3%)
  between operations  13.6 us (3%)
    all_to_all x1, blocking collectives, body(): lax.all_to_all(outgoing, 'expert', split_axis=0, concat_axis=0, tiled=True)  108 us
    all_to_all x1, waiting for transfers between devices, body(): lax.all_to_all(results.reshape(source_count, slot_count, width), 'expert'...  104 us
    all_to_all x1, waiting for transfers between devices, body(): lax.all_to_all(query_items, 'expert', split_axis=1, concat_axis=0, tiled=...  34.7 us
    all_to_all x1, waiting for transfers between devices, body(): lax.all_to_all(key_items, 'expert', split_axis=1, concat_axis=0, tiled=True)  29.9 us
    all_to_all x1, waiting for transfers between devices, body(): lax.all_to_all(value_items, 'expert', split_axis=1, concat_axis=0, tiled=...  14.1 us
    gather x1, local copies, waits for them, and re-layouts, body(): returned.reshape(expert_count * capacity, model_width)[target]  10 us
    dot_general x2, matrix products, one_block(): jnp.einsum('iqk,kid->qid', weights, value_items, preferred_element_type=j...  9.9 us
  transfers between devices with their start and end apart: 6, of which 5 were waited for; matrix products, arithmetic and copies ran while one was open for 13% of the time, Pallas kernels for 0%

commit v1 on v0

--- a/solution.py
+++ b/solution.py
@@ -69,7 +69,6 @@
     half_rows, stream_count, query_width = queries.shape
     model_width = residual.shape[2]
     token_rows = half_rows * stream_count
-    pair_count = token_rows * TOP
     expert_count = lax.axis_size("expert")
     item_count = stream_count * HEADS // expert_count
     key_heads = jnp.concatenate(
@@ -82,11 +81,12 @@
     query_items = queries.reshape(half_rows, stream_count * HEADS, NOPE + ROPE)
     key_items = key_heads.reshape(half_rows, stream_count * HEADS, NOPE + ROPE)
     value_items = values.reshape(half_rows, stream_count * HEADS, V_DIM)
-    query_all, key_all, value_all = (
-        lax.all_to_all(query_items, "expert", split_axis=1, concat_axis=0, tiled=True),
-        lax.all_to_all(key_items, "expert", split_axis=1, concat_axis=0, tiled=True),
-        lax.all_to_all(value_items, "expert", split_axis=1, concat_axis=0, tiled=True),
-    )
+    packed = jnp.concatenate([query_items, key_items, value_items], axis=2)
+    packed_all = lax.all_to_all(packed, "expert", split_axis=1, concat_axis=0, tiled=True)
+    qk_width = NOPE + ROPE
+    query_all = packed_all[:, :, :qk_width]
+    key_all = packed_all[:, :, qk_width : 2 * qk_width]
+    value_all = packed_all[:, :, 2 * qk_width :]
     item_ids = lax.axis_index("expert") * item_count + jnp.arange(item_count, dtype=jnp.int32)
     stream_ids = item_ids // HEADS
     selector = (stream_ids[:, None] == jnp.arange(stream_count, dtype=jnp.int32)[None, :]).astype(
@@ -108,40 +108,24 @@
     normed = (hidden * lax.rsqrt(mean_square + EPSILON) * norm_gain.astype(jnp.float32)).astype(
         jnp.bfloat16
     )
-    capacity = min(token_rows, max(2, token_rows * TOP * 3 // (2 * expert_count)))
-    flat_routes = routes.reshape(pair_count)
-    matches = (flat_routes[:, None] == jnp.arange(expert_count, dtype=jnp.int32)[None, :]).astype(
-        jnp.int32
+    token_routes = routes.reshape(token_rows, TOP)
+    token_weights = route_weights.reshape(token_rows, TOP)
+    expert_ids = jnp.arange(expert_count, dtype=jnp.int32)
+    weight_table = jnp.sum(
+        jnp.where(
+            token_routes[:, :, None] == expert_ids[None, None, :], token_weights[:, :, None], 0.0
+        ),
+        axis=1,
     )
-    earlier = jnp.cumsum(matches, axis=0) - matches
-    slot_rank = jnp.sum(earlier * matches, axis=1)
-    target = flat_routes * capacity + slot_rank
-    pair_ids = jnp.arange(pair_count, dtype=jnp.int32)
-    slot_source = (
-        jnp.full((expert_count * capacity,), pair_count, jnp.int32).at[target].set(pair_ids)
+    own_weights = lax.all_to_all(
+        weight_table.T, "expert", split_axis=0, concat_axis=0, tiled=True
+    ).reshape(expert_count * token_rows, 1)
+    all_rows = lax.all_gather(normed, "expert", axis=0, tiled=True)
+    results = feed_forward(all_rows, expert_gate[0], expert_up[0], expert_down[0])
+    partial = (own_weights * results.astype(jnp.float32)).astype(jnp.bfloat16)
+    routed_sum = lax.psum_scatter(partial, "expert", scatter_dimension=0, tiled=True).astype(
+        jnp.float32
     )
-    slot_live = slot_source < pair_count
-    slot_rows = normed[jnp.minimum(slot_source, pair_count - 1) // TOP]
-    outgoing = jnp.where(slot_live[:, None], slot_rows, jnp.zeros_like(slot_rows)).reshape(
-        expert_count, capacity, model_width
-    )
-    gate_matrix = expert_gate[0]
-    up_matrix = expert_up[0]
-    down_matrix = expert_down[0]
-    arrived = lax.all_to_all(outgoing, "expert", split_axis=0, concat_axis=0, tiled=True)
-    source_count, slot_count, width = arrived.shape
-    flat_rows = arrived.reshape(source_count * slot_count, width)
-    results = feed_forward(flat_rows, gate_matrix, up_matrix, down_matrix)
-    returned = lax.all_to_all(
-        results.reshape(source_count, slot_count, width),
-        "expert",
-        split_axis=0,
-        concat_axis=0,
-        tiled=True,
-    )
-    pair_outputs = returned.reshape(expert_count * capacity, model_width)[target]
-    weighted = route_weights.reshape(pair_count, 1) * pair_outputs.astype(jnp.float32)
-    routed_sum = jnp.sum(weighted.reshape(token_rows, TOP, model_width), axis=1)
     layer_out = (hidden + routed_sum).astype(jnp.bfloat16)
     return layer_out.reshape(half_rows, stream_count, model_width)
 

time: 451 us -> 369 us (0.82)
  blocking collectives: 108 us -> 0 us
  waiting for transfers between devices: 190 us -> 247 us
  local copies, waits for them, and re-layouts: 60.4 us -> 29 us
  matrix products: 35.2 us -> 51.9 us
  starting transfers between devices: 26.8 us -> 17.8 us
  other arithmetic: 13.9 us -> 6.21 us
    all_to_all x4 -> x2, waiting for transfers between devices: 182 us -> 65.2 us  [the longest x1 65.2 us: body(): lax.all_to_all(packed, 'expert', split_axis=1, concat_axis=0, tiled=True)]
    all_to_all x1 -> x0, blocking collectives: 108 us -> none  [body(): lax.all_to_all(outgoing, 'expert', split_axis=0, concat_axis=0, tiled=True)]
    reduce_scatter x0 -> x1, waiting for transfers between devices: none -> 103 us  [body(): lax.psum_scatter(partial, 'expert', scatter_dimension=0, tiled=True)]
    all_gather x0 -> x1, waiting for transfers between devices: none -> 67.4 us  [body(): all_rows = lax.all_gather(normed, 'expert', axis=0, tiled=True)]
    gather x2 -> x0, local copies, waits for them, and re-layouts: 16 us -> none  [the longest x1 10 us: body(): returned.reshape(expert_count * capacity, model_width)[target]]
    dot_general x1, matrix products: 5.6 us -> 19 us  [feed_forward(): jnp.dot(activated, down_matrix, preferred_element_type=jnp.float32)]
    all_to_all x4 -> x2, starting transfers between devices: 21.9 us -> 11.4 us  [the longest x1 6.52 us: body(): lax.all_to_all(packed, 'expert', split_axis=1, concat_axis=0, tiled=True)]
    dot_general x1, matrix products: 4 us -> 11.2 us  [feed_forward(): gate_part = jnp.dot(rows, gate_matrix, preferred_element_type=jnp.float32)]
  transfers between devices with their start and end apart: 6 -> 6, of which waited for: 5 -> 4; matrix products, arithmetic and copies ran while one was open for 13% -> 16% of each run, Pallas kernels for 0% -> 0%
where the time goes in v1:
time: 369 us; the launch traced here: 367 us
  waiting for transfers between devices  247 us (67%)
  matrix products  51.9 us (14%)
  local copies, waits for them, and re-layouts  29 us (8%)
  starting transfers between devices  17.8 us (5%)
  between operations  13.3 us (4%)
  other arithmetic  6.21 us (2%)
    reduce_scatter x1, waiting for transfers between devices, body(): lax.psum_scatter(partial, 'expert', scatter_dimension=0, tiled=True)  103 us
    all_gather x1, waiting for transfers between devices, body(): all_rows = lax.all_gather(normed, 'expert', axis=0, tiled=True)  67.4 us
    all_to_all x1, waiting for transfers between devices, body(): lax.all_to_all(packed, 'expert', split_axis=1, concat_axis=0, tiled=True)  65.2 us
    dot_general x1, matrix products, feed_forward(): jnp.dot(activated, down_matrix, preferred_element_type=jnp.float32)  19 us
    all_to_all x1, waiting for transfers between devices, body(): lax.all_to_all(attended_items, 'expert', split_axis=0, concat_axis=1, til...  11.3 us
    dot_general x1, matrix products, feed_forward(): gate_part = jnp.dot(rows, gate_matrix, preferred_element_type=jnp.float32)  11.2 us
    dot_general x2, matrix products, one_block(): jnp.einsum('iqk,kid->qid', weights, value_items, preferred_element_type=j...  9.99 us
  transfers between devices with their start and end apart: 6, of which 4 were waited for; matrix products, arithmetic and copies ran while one was open for 16% of the time, Pallas kernels for 0%

profile of v1, /device:TPU:15, one launch (start us, length us, event | category | flops | bytes accessed | tf_op | source)
XLA Modules:
  0.0 366.9 jit_solution(16505499068747133357)
XLA Ops:
  8.8 2.2 reshape.126
  10.9 3.4 reshape.125
  14.4 2.3 pad_maximum_fusion
  16.7 2.5 copy.42
  19.2 6.5 %all-to-all-start = ((bf16[64,32,512]{2,0,1:T(8,128)(2,1)}), bf16[64,32,512]{2,0,1:T(8,128)(2,1)}, u32[]{:S(2)}, u32[]{:S(2)}) async-start(bf16[64,32,512]{2,0,1:T(8,128)(2,1)} %copy.42), calls=%async_computation | async-start | bytes 4194304 | tf_op jit(solution)/shard_map/all_to_all | solution.py:85
  25.9 65.2 %all-to-all-done = bf16[64,32,512]{2,0,1:T(8,128)(2,1)} async-done(((bf16[64,32,512]{2,0,1:T(8,128)(2,1)}), bf16[64,32,512]{2,0,1:T(8,128)(2,1)}, u32[]{:S(2)}, u32[]{:S(2)}) %all-to-all-start) | async-done | bytes 2097184 | tf_op jit(solution)/shard_map/all_to_all | solution.py:85
  91.1 1.8 copy.43
  95.6 2.2 copy.45
  97.8 2.2 copy.44
  100.0 20.0 %while.11 = (s32[]{:T(128)}, bf16[2,512,2,128]{3,1,0,2:T(8,128)(2,1)}, s32[2]{0:T(128)S(1)}, s32[2,1024]{1,0:T(2,128)S(1)}, bf16[1024,2,192]{0,2,1:T(8,128)(2,1)...) while((s32[]{:T(128)}, ...), condition=%wide.region_4.5_spmd.clone, body=%wide.region_1.4_spmd.clone.sunk | while | flops 1088032256 | bytes 4763843 | solution.py:50
  101.6 3.4 fusion.67
  105.0 5.0 %fusion.68 = bf16[2,512,2,128]{3,1,0,2:T(8,128)(2,1)} fusion(bf16[2,512,2,128]{3,1,0,2:T(8,128)(2,1)} %get-tuple-element.172, s32[]{:T(128)S(6)} %copy.63, bf16[1024,2,128]{2,0,1:T(8,128)(2,1)} %get-tuple-element.188, f32[2,512]{1,0:T(2,128)S(1)} %fusion.67, s32[2,1024]{1,0:T(2,128)S(1)} %get-tuple-element.185, ...), kind=kOutput, calls=%fused_computation.15.clone.1 | convolution fusion | flops 678561792 | bytes 2506760 | tf_op jit(solution)/shard_map/while/body/eval_jaxpr/iqk,kid->qid/dot_general | solution.py:46
  111.6 3.4 fusion.67
  115.0 5.0 %fusion.68 = bf16[2,512,2,128]{3,1,0,2:T(8,128)(2,1)} fusion(bf16[2,512,2,128]{3,1,0,2:T(8,128)(2,1)} %get-tuple-element.172, s32[]{:T(128)S(6)} %copy.63, bf16[1024,2,128]{2,0,1:T(8,128)(2,1)} %get-tuple-element.188, f32[2,512]{1,0:T(2,128)S(1)} %fusion.67, s32[2,1024]{1,0:T(2,128)S(1)} %get-tuple-element.185, ...), kind=kOutput, calls=%fused_computation.15.clone.1 | convolution fusion | flops 678561792 | bytes 2506760 | tf_op jit(solution)/shard_map/while/body/eval_jaxpr/iqk,kid->qid/dot_general | solution.py:46
  120.0 2.4 copy.47
  122.3 6.1 %all-to-all-start.1 = ((bf16[1024,2,128]{2,1,0:T(2,128)(2,1)}), bf16[1024,2,128]{2,1,0:T(2,128)(2,1)S(1)}, u32[]{:S(2)}, u32[]{:S(2)}) async-start(bf16[1024,2,128]{2,1,0:T(2,128)(2,1)} %copy.47), calls=%async_computation.1 | async-start | bytes 1048576 | tf_op jit(solution)/shard_map/all_to_all | solution.py:97
  128.5 2.2 reshape.130
  130.7 11.3 %all-to-all-done.1 = bf16[1024,2,128]{2,1,0:T(2,128)(2,1)S(1)} async-done(((bf16[1024,2,128]{2,1,0:T(2,128)(2,1)}), bf16[1024,2,128]{2,1,0:T(2,128)(2,1)S(1)}, u32[]{:S(2)}, u32[]{:S(2)}) %all-to-all-start.1) | async-done | bytes 524320 | tf_op jit(solution)/shard_map/all_to_all | solution.py:97
  144.6 5.0 %multiply_reduce_fusion = (f32[128]{0:T(128)S(1)}, f32[128,2048]{1,0:T(8,128)S(1)}) fusion(f32[128,2048]{1,0:T(8,128)} %reshape.130, bf16[128,2048]{1,0:T(8,128)(2,1)S(1)} %reshape.128, bf16[2048,2048]{1,0:T(8,128)(2,1)} %all-gather.3.cloned.1.call-done), kind=kOutput, calls=%fused_computation.40 | convolution fusion | flops 1074528128 | bytes 11010560 | tf_op jit(solution)/shard_map/dot_general | solution.py:101
  152.2 4.9 %all-to-all-start.2 = ((f32[16,1,128]{2,1,0:T(1,128)}), f32[16,1,128]{2,1,0:T(1,128)S(1)}, u32[]{:S(2)}, u32[]{:S(2)}) async-start(f32[16,1,128]{2,1,0:T(1,128)} %bitcast.9), calls=%async_computation.2 | async-start | bytes 16384 | tf_op jit(solution)/shard_map/all_to_all | solution.py:120
  157.4 67.4 %all-gather.5.cloned.1.call-done = bf16[2048,2048]{1,0:T(8,128)(2,1)} async-done(((bf16[128,2048]{1,0:T(8,128)(2,1)}), bf16[2048,2048]{1,0:T(8,128)(2,1)}) %all-gather.5.cloned.1.call-update) | async-done | bytes 8388624 | tf_op jit(solution)/shard_map/all_gather | solution.py:123
  224.8 11.2 %fusion.40 = f32[2048,704]{0,1:T(8,128)} fusion(bf16[2048,2048]{1,0:T(8,128)(2,1)} %all-gather.5.cloned.1.call-done, bf16[1,2048,704]{1,2,0:T(8,128)(2,1)} %param.23), kind=kOutput, calls=%fused_computation.33 | convolution fusion | flops 5905580032 | bytes 17039360 | tf_op jit(solution)/shard_map/dot_general | solution.py:18
  235.9 19.0 %multiply_convert_fusion = bf16[2048,2048]{1,0:T(8,128)(2,1)} fusion(f32[2048]{0:T(1024)S(1)} %bitcast.66, f32[2048,704]{0,1:T(8,128)} %fusion.40, bf16[2048,2048]{1,0:T(8,128)(2,1)} %all-gather.5.cloned.1.call-done, bf16[1,704,2048]{2,1,0:T(8,128)(2,1)S(1)} %copy-done, bf16[1,2048,704]{1,2,0:T(8,128)(2,1)} %param.24), kind=kOutput, calls=%fused_computation.29 | convolution fusion | flops 11836588032 | bytes 28319744 | tf_op jit(solution)/shard_map/dot_general | solution.py:21
  255.0 102.8 %reduce-scatter.2.cloned.1.call-done = bf16[128,2048]{1,0:T(8,128)(2,1)} async-done(((bf16[2048,2048]{1,0:T(8,128)(2,1)}), bf16[128,2048]{1,0:T(8,128)(2,1)}) %reduce-scatter.2.cloned.1.call-update) | async-done | bytes 524304 | tf_op jit(solution)/shard_map/reduce_scatter | solution.py:126
  (49 shorter events, 15.2 us)
Async XLA Ops:
  6.5 229.4 %copy-start = (bf16[1,704,2048]{2,1,0:T(8,128)(2,1)S(1)}, bf16[1,704,2048]{2,1,0:T(8,128)(2,1)}, u32[]{:S(2)}) copy-start(bf16[1,704,2048]{2,1,0:T(8,128)(2,1)} %param.25) | copy-start | bytes 8650756
  6.5 7.8 %copy-start.2 = (bf16[64,2,64]{2,1,0:T(2,128)(2,1)S(1)}, bf16[64,2,64]{2,1,0:T(2,128)(2,1)}, u32[]{:S(2)}) copy-start(bf16[64,2,64]{2,1,0:T(2,128)(2,1)} %param.17) | copy-start | bytes 49156
  6.5 138.1 %all-gather.3.cloned.1.call-start = ((), (), s32[]{:S(2)}) async-start(), calls=%async_computation.4 | async-start | bytes 8650752 | tf_op jit(solution)/shard_map/all_gather | solution.py:103
  16.7 9.1 %copy-start.3 = (s32[2,1024]{1,0:T(2,128)S(1)}, s32[2,1024]{1,0:T(2,128)}, u32[]{:S(2)}) copy-start(s32[2,1024]{1,0:T(2,128)} %param.20) | copy-start | bytes 24580
  19.2 71.9 %all-to-all-start = ((bf16[64,32,512]{2,0,1:T(8,128)(2,1)}), bf16[64,32,512]{2,0,1:T(8,128)(2,1)}, u32[]{:S(2)}, u32[]{:S(2)}) async-start(bf16[64,32,512]{2,0,1:T(8,128)(2,1)} %copy.42), calls=%async_computation | async-start | bytes 4194304 | tf_op jit(solution)/shard_map/all_to_all | solution.py:85
  100.0 28.5 %copy-start.4 = (bf16[2048]{0:T(1024)(128)(2,1)S(1)}, bf16[2048]{0:T(1024)(128)(2,1)}, u32[]{:S(2)}) copy-start(bf16[2048]{0:T(1024)(128)(2,1)} %param.22) | copy-start | bytes 12292
  122.3 19.6 %all-to-all-start.1 = ((bf16[1024,2,128]{2,1,0:T(2,128)(2,1)}), bf16[1024,2,128]{2,1,0:T(2,128)(2,1)S(1)}, u32[]{:S(2)}, u32[]{:S(2)}) async-start(bf16[1024,2,128]{2,1,0:T(2,128)(2,1)} %copy.47), calls=%async_computation.1 | async-start | bytes 1048576 | tf_op jit(solution)/shard_map/all_to_all | solution.py:97
  128.4 96.3 %all-gather.5.cloned.1.call-start = ((), (), s32[]{:S(2)}) async-start(), calls=%async_computation.5 | async-start | bytes 8912896 | tf_op jit(solution)/shard_map/all_gather | solution.py:123
  144.6 7.0 %copy-start.5 = (s32[1,1,128,6]{2,1,3,0:T(1,128)S(1)}, s32[1,1,128,6]{2,1,3,0:T(1,128)}, u32[]{:S(2)}) copy-start(s32[1,1,128,6]{2,1,3,0:T(1,128)} %param.26) | copy-start | bytes 9220
  144.6 7.0 %copy-start.6 = (f32[1,1,128,6]{2,1,3,0:T(1,128)S(1)}, f32[1,1,128,6]{2,1,3,0:T(1,128)}, u32[]{:S(2)}) copy-start(f32[1,1,128,6]{2,1,3,0:T(1,128)} %param.27) | copy-start | bytes 9220
  149.6 1.0 copy-start.1
  152.2 83.7 %all-to-all-start.2 = ((f32[16,1,128]{2,1,0:T(1,128)}), f32[16,1,128]{2,1,0:T(1,128)S(1)}, u32[]{:S(2)}, u32[]{:S(2)}) async-start(f32[16,1,128]{2,1,0:T(1,128)} %bitcast.9), calls=%async_computation.2 | async-start | bytes 16384 | tf_op jit(solution)/shard_map/all_to_all | solution.py:120
  157.1 200.6 %reduce-scatter.2.cloned.1.call-start = ((), (), s32[]{:S(2)}) async-start(), calls=%async_computation.6 | async-start | bytes 8912896 | tf_op jit(solution)/shard_map/reduce_scatter | solution.py:126
Sparse Core Ops, SparseCore 0:
  10.2 103.3 all-gather.2
  151.7 73.0 all-gather.4
  255.1 102.5 reduce-scatter.1

commit v2 on v1

v2 whole, which is shorter than its diff:
```python
import jax
import jax.numpy as jnp
from jax import lax
from jax.experimental import pallas as pl
from jax.experimental.pallas import tpu as pltpu
from jax.sharding import PartitionSpec as P

HEADS = 16
NOPE = 128
ROPE = 64
V_DIM = 128
TOP = 6


EPSILON = 1e-06
QUERY_BLOCK = 256
CHUNKS = 2
ITEM_WIDTH = 2 * (NOPE + ROPE) + V_DIM


def feed_forward(rows, gate_matrix, up_matrix, down_matrix):
    gate_part = jnp.dot(rows, gate_matrix, preferred_element_type=jnp.float32)
    up_part = jnp.dot(rows, up_matrix, preferred_element_type=jnp.float32)
    activated = (jax.nn.silu(gate_part) * up_part).astype(jnp.bfloat16)
    return jnp.dot(activated, down_matrix, preferred_element_type=jnp.float32).astype(jnp.bfloat16)


def attend_kernel(packed_ref, segment_row_ref, segment_column_ref, attended_ref):
    length, packed_width = packed_ref.shape
    block_rows = min(QUERY_BLOCK, length)
    score_scale = (NOPE + ROPE) ** (-0.5)
    contract_last = (((1,), (1,)), ((), ()))
    for item in range(packed_width // ITEM_WIDTH):
        base = item * ITEM_WIDTH
        for first_row in range(0, length, block_rows):
            key_count = first_row + block_rows
            rows = pl.ds(first_row, block_rows)
            keys = pl.ds(0, key_count)
            rope_at = base + 2 * NOPE + V_DIM
            query_rope = packed_ref[rows, rope_at : rope_at + 2 * ROPE][:, :ROPE]
            key_rope = packed_ref[keys, rope_at : rope_at + 2 * ROPE][:, ROPE:]
            scores = lax.dot_general(
                packed_ref[rows, base : base + NOPE],
                packed_ref[keys, base + NOPE : base + 2 * NOPE],
                contract_last,
                preferred_element_type=jnp.float32,
            ) + lax.dot_general(
                query_rope, key_rope, contract_last, preferred_element_type=jnp.float32
            )
            scores = scores * score_scale
            row_positions = first_row + lax.broadcasted_iota(jnp.int32, scores.shape, 0)
            key_positions = lax.broadcasted_iota(jnp.int32, scores.shape, 1)
            allowed = (row_positions >= key_positions) & (
                segment_column_ref[rows, :] == segment_row_ref[:, keys]
            )
            scores = jnp.where(allowed, scores, -jnp.inf)
            row_peak = jnp.max(scores, axis=1, keepdims=True)
            raised = jnp.exp(scores - row_peak)
            weights = (raised / jnp.sum(raised, axis=1, keepdims=True)).astype(jnp.bfloat16)
            attended_ref[rows, item * V_DIM : (item + 1) * V_DIM] = jnp.dot(
                weights,
                packed_ref[keys, base + 2 * NOPE : base + 2 * NOPE + V_DIM],
                preferred_element_type=jnp.float32,
            ).astype(jnp.bfloat16)


def attend_items(packed_rows, segment_row):
    length, packed_width = packed_rows.shape
    item_count = packed_width // ITEM_WIDTH
    vmem = pl.BlockSpec(memory_space=pltpu.VMEM)
    return pl.pallas_call(
        attend_kernel,
        out_shape=jax.ShapeDtypeStruct((length, item_count * V_DIM), jnp.bfloat16),
        in_specs=[vmem] * 3,
        out_specs=vmem,
        cost_estimate=pl.CostEstimate(
            flops=item_count * length * length * (NOPE + ROPE + V_DIM),
            bytes_accessed=2 * length * packed_width,
            transcendentals=item_count * length * length // 2,
        ),
    )(packed_rows, segment_row.reshape(1, length), segment_row.reshape(length, 1))


def body(
    queries,
    key_nope,
    key_rope,
    values,
    residual,
    segments,
    out_proj,
    norm_gain,
    expert_gate,
    expert_up,
    expert_down,
    routes,
    route_weights,
):
    half_rows, stream_count, query_width = queries.shape
    model_width = residual.shape[2]
    token_rows = half_rows * stream_count
    expert_count = lax.axis_size("expert")
    item_count = stream_count * HEADS // expert_count
    query_heads = queries.reshape(half_rows, stream_count, HEADS, NOPE + ROPE)
    head_shape = (half_rows, stream_count, HEADS, ROPE)
    packed = jnp.concatenate(
        [
            query_heads[..., :NOPE],
            key_nope.reshape(half_rows, stream_count, HEADS, NOPE),
            values.reshape(half_rows, stream_count, HEADS, V_DIM),
            query_heads[..., NOPE:],
            jnp.broadcast_to(key_rope[:, :, None, :], head_shape),
        ],
        axis=3,
    ).reshape(half_rows, expert_count, item_count * ITEM_WIDTH)
    packed_all = lax.all_to_all(
        packed.transpose(1, 0, 2), "expert", split_axis=0, concat_axis=0, tiled=True
    )
    length = expert_count * half_rows
    own_stream = lax.axis_index("expert") * item_count // HEADS
    selector = (jnp.arange(stream_count, dtype=jnp.int32) == own_stream).astype(jnp.int32)
    segment_row = jnp.sum(selector[:, None] * segments, axis=0)
    attended_items = attend_items(
        packed_all.reshape(length, item_count * ITEM_WIDTH), segment_row
    )
    attended_back = lax.all_to_all(
        attended_items.reshape(expert_count, half_rows, item_count * V_DIM),
        "expert",
        split_axis=0,
        concat_axis=0,
        tiled=True,
    )
    attn_rows = (
        attended_back.reshape(
            stream_count, expert_count // stream_count, half_rows, item_count * V_DIM
        )
        .transpose(2, 0, 1, 3)
        .reshape(token_rows, HEADS * V_DIM)
    )
    projected = jnp.dot(
        attn_rows,
        lax.all_gather(out_proj, ("dp", "expert"), axis=0, tiled=True),
        preferred_element_type=jnp.float32,
    )
    hidden = residual.reshape(token_rows, model_width).astype(jnp.float32) + projected
    mean_square = jnp.mean(hidden * hidden, axis=1, keepdims=True)
    normed = (hidden * lax.rsqrt(mean_square + EPSILON) * norm_gain.astype(jnp.float32)).astype(
        jnp.bfloat16
    )
    token_routes = routes.reshape(token_rows, TOP)
    token_weights = route_weights.reshape(token_rows, TOP)
    expert_ids = jnp.arange(expert_count, dtype=jnp.int32)
    weight_table = jnp.sum(
        jnp.where(
            token_routes[:, :, None] == expert_ids[None, None, :], token_weights[:, :, None], 0.0
        ),
        axis=1,
    )
    own_weights = lax.all_to_all(
        weight_table.T, "expert", split_axis=0, concat_axis=0, tiled=True
    ).reshape(expert_count, token_rows)
    chunk_rows = token_rows // CHUNKS
    routed_chunks = []
    for chunk in range(CHUNKS):
        part = slice(chunk * chunk_rows, (chunk + 1) * chunk_rows)
        all_rows = lax.all_gather(normed[part], "expert", axis=0, tiled=True)
        results = feed_forward(all_rows, expert_gate[0], expert_up[0], expert_down[0])
        scale = own_weights[:, part].reshape(expert_count * chunk_rows, 1)
        partial = (scale * results.astype(jnp.float32)).astype(jnp.bfloat16)
        routed_chunks.append(
            lax.psum_scatter(partial, "expert", scatter_dimension=0, tiled=True)
        )
    routed_sum = jnp.concatenate(routed_chunks, axis=0).astype(jnp.float32)
    layer_out = (hidden + routed_sum).astype(jnp.bfloat16)
    return layer_out.reshape(half_rows, stream_count, model_width)


def solution(mesh):
    return jax.shard_map(
        body,
        mesh=mesh,
        in_specs=(
            P("expert", "dp", None),
            P("expert", "dp", None),
            P("expert", "dp", None),
            P("expert", "dp", None),
            P("expert", "dp", None),
            P("dp", None),
            P(("dp", "expert"), None),
            P(),
            P("expert", None, None),
            P("expert", None, None),
            P("expert", None, None),
            P("dp", "expert", None, None),
            P("dp", "expert", None, None),
        ),
        out_specs=P("expert", "dp", None),
        check_vma=False,
    )
```

time: 369 us -> 416 us (1.13)
  waiting for transfers between devices: 247 us -> 294 us
  blocking collectives: 0 us -> 8.53 us
  matrix products: 51.9 us -> 43.8 us
  Pallas kernels: 0 us -> 7.98 us
  starting transfers between devices: 17.8 us -> 11.7 us
  other arithmetic: 6.21 us -> 1.71 us
    reduce_scatter x1 -> x2, waiting for transfers between devices: 103 us -> 130 us  [body(): lax.psum_scatter(partial, 'expert', scatter_dimension=0, tiled=True)]
    all_to_all x3 -> x2, waiting for transfers between devices: 76.5 us -> 91.3 us  [the longest x1 80 us: body(): lax.all_to_all(packed.transpose(1, 0, 2), 'expert', split_axis=0, concat_...]
    all_to_all x0 -> x1, blocking collectives: none -> 8.53 us  [body(): lax.all_to_all(weight_table.T, 'expert', split_axis=0, concat_axis=0, til...]
    pallas_call x0 -> x1, Pallas kernels: none -> 7.98 us  [attend_items(): pl.pallas_call(attend_kernel, out_shape=jax.ShapeDtypeStruct((length, ite...]
    sub x2 -> x0, matrix products: 6.76 us -> none  [one_block(): raised = jnp.exp(scores - row_peak)]
    all_to_all x3 -> x2, starting transfers between devices: 17.5 us -> 11.3 us  [the longest x1 6.64 us: body(): lax.all_to_all(packed.transpose(1, 0, 2), 'expert', split_axis=0, concat_...]
    dot_general x3 -> x2, matrix products: 21.1 us -> 15.7 us  [feed_forward(): up_part = jnp.dot(rows, up_matrix, preferred_element_type=jnp.float32)]
    unnamed x18 -> x19, local copies, waits for them, and re-layouts: 5.4 us -> 1.1 us
  transfers between devices with their start and end apart: 6 -> 7, of which waited for: 4 -> 6; matrix products, arithmetic and copies ran while one was open for 16% -> 16% of each run, Pallas kernels for 0% -> 2%
where the time goes in v2:
time: 416 us; the launch traced here: 411 us
  waiting for transfers between devices  294 us (71%)
  matrix products  43.8 us (11%)
  local copies, waits for them, and re-layouts  30.7 us (7%)
  between operations  13.3 us (3%)
  starting transfers between devices  11.7 us (3%)
  blocking collectives  8.53 us (2%)
  Pallas kernels  7.98 us (2%)
    reduce_scatter x2, waiting for transfers between devices, body(): lax.psum_scatter(partial, 'expert', scatter_dimension=0, tiled=True)  130 us
    all_to_all x1, waiting for transfers between devices, body(): lax.all_to_all(packed.transpose(1, 0, 2), 'expert', split_axis=0, concat_...  80 us
    all_gather x2, waiting for transfers between devices, body(): all_rows = lax.all_gather(normed[part], 'expert', axis=0, tiled=True)  71.4 us
    dot_general x2, matrix products, feed_forward(): jnp.dot(activated, down_matrix, preferred_element_type=jnp.float32)  23.1 us
    dot_general x2, matrix products, feed_forward(): up_part = jnp.dot(rows, up_matrix, preferred_element_type=jnp.float32)  15.7 us
    all_to_all x1, waiting for transfers between devices, body(): lax.all_to_all(attended_items.reshape(expert_count, half_rows, item_count...  11.3 us
    all_to_all x1, blocking collectives, body(): lax.all_to_all(weight_table.T, 'expert', split_axis=0, concat_axis=0, til...  8.53 us
  transfers between devices with their start and end apart: 7, of which 6 were waited for; matrix products, arithmetic and copies ran while one was open for 16% of the time, Pallas kernels for 2%

profile of v2, /device:TPU:15, one launch (start us, length us, event | category | flops | bytes accessed | tf_op | source)
XLA Modules:
  0.0 411.5 jit_solution(14672491597301067962)
XLA Ops:
  7.3 3.5 reshape.59
  10.8 1.9 slice.25
  12.7 2.2 reshape.60
  14.9 2.2 reshape.61
  17.9 5.0 %concatenate.6 = bf16[64,2,16,512]{3,2,1,0:T(8,128)(2,1)} concatenate(bf16[64,2,16,128]{3,2,1,0:T(8,128)(2,1)S(1)} %slice-done, bf16[64,2,16,128]{3,2,1,0:T(8,128)(2,1)} %reshape.60, bf16[64,2,16,128]{3,2,1,0:T(8,128)(2,1)} %reshape.61, bf16[64,2,16,64]{3,2,1,0:T(8,128)(2,1)} %slice.25, bf16[64,2,16,64]{3,2,1,0:T(8,128)(2,1)} %broadcast_in_dim.24), dimensions={3} | concatenate | bytes 4194304 | tf_op jit(solution)/shard_map/concatenate | solution.py:106
  22.9 4.1 reshape.62
  27.0 4.1 copy.26
  31.1 6.6 %all-to-all-start = ((bf16[16,64,1024]{2,1,0:T(8,128)(2,1)}), bf16[16,64,1024]{2,1,0:T(8,128)(2,1)}, u32[]{:S(2)}, u32[]{:S(2)}) async-start(bf16[16,64,1024]{2,1,0:T(8,128)(2,1)} %copy.26), calls=%async_computation | async-start | bytes 4194304 | tf_op jit(solution)/shard_map/all_to_all | solution.py:116
  38.9 80.0 %all-to-all-done = bf16[16,64,1024]{2,1,0:T(8,128)(2,1)} async-done(((bf16[16,64,1024]{2,1,0:T(8,128)(2,1)}), bf16[16,64,1024]{2,1,0:T(8,128)(2,1)}, u32[]{:S(2)}, u32[]{:S(2)}) %all-to-all-start) | async-done | bytes 2097184 | tf_op jit(solution)/shard_map/all_to_all | solution.py:116
  118.9 8.0 %shard_map.127 = bf16[1024,256]{1,0:T(8,128)(2,1)} custom-call(bf16[1024,1024]{1,0:T(8,128)(2,1)} %bitcast.1.packed_ref, s32[1,1024]{1,0:T(1,128)} %bitcast.60, s32[1024,1]{1,0:T(8,128)} %copy.27.segment_column_ref), custom_call_target="tpu_custom_call" | custom-call | flops 671088640 | bytes 2097152 | tf_op jit(solution)/shard_map/pallas_call | solution.py:71
  126.9 4.7 %all-to-all-start.1 = ((bf16[16,64,256]{2,1,0:T(8,128)(2,1)}), bf16[16,64,256]{2,1,0:T(8,128)(2,1)S(1)}, u32[]{:S(2)}, u32[]{:S(2)}) async-start(bf16[16,64,256]{2,1,0:T(8,128)(2,1)} %bitcast.57), calls=%async_computation.1 | async-start | bytes 1048576 | tf_op jit(solution)/shard_map/all_to_all | solution.py:126
  131.7 2.2 reshape.70
  133.9 11.3 %all-to-all-done.1 = bf16[16,64,256]{2,1,0:T(8,128)(2,1)S(1)} async-done(((bf16[16,64,256]{2,1,0:T(8,128)(2,1)}), bf16[16,64,256]{2,1,0:T(8,128)(2,1)S(1)}, u32[]{:S(2)}, u32[]{:S(2)}) %all-to-all-start.1) | async-done | bytes 524320 | tf_op jit(solution)/shard_map/all_to_all | solution.py:126
  145.6 5.0 %multiply_reduce_fusion = (f32[128]{0:T(128)S(1)}, f32[128,2048]{1,0:T(8,128)S(1)}) fusion(f32[128,2048]{1,0:T(8,128)} %reshape.70, bf16[128,2048]{1,0:T(8,128)(2,1)S(1)} %bitcast.55, bf16[2048,2048]{1,0:T(8,128)(2,1)} %all-gather.4.cloned.1.call-done), kind=kOutput, calls=%fused_computation.17 | convolution fusion | flops 1074528128 | bytes 11010560 | tf_op jit(solution)/shard_map/dot_general | solution.py:140
  153.5 8.5 %all_to_all.22 = f32[16,1,128]{2,1,0:T(1,128)S(1)} all-to-all(f32[16,1,128]{2,1,0:T(1,128)S(1)} %bitcast.61), channel_id=1, replica_groups=mesh['dp'=2,'expert'=16] {'expert'}, dimensions={0} | all-to-all | bytes 16384 | tf_op jit(solution)/shard_map/all_to_all | solution.py:159
  162.1 40.0 %all-gather.6.cloned.1.call-done = bf16[1024,2048]{1,0:T(8,128)(2,1)} async-done(((bf16[64,2048]{1,0:T(8,128)(2,1)}), bf16[1024,2048]{1,0:T(8,128)(2,1)}) %all-gather.6.cloned.1.call-update) | async-done | bytes 4194320 | tf_op jit(solution)/shard_map/all_gather | solution.py:166
  202.2 7.8 %fusion.4 = f32[1024,704]{0,1:T(8,128)} fusion(bf16[1024,2048]{1,0:T(8,128)(2,1)} %all-gather.6.cloned.1.call-done, bf16[1,2048,704]{1,2,0:T(8,128)(2,1)} %param.22), kind=kOutput, calls=%fused_computation.6 | convolution fusion | flops 2952790016 | bytes 9961472 | tf_op jit(solution)/shard_map/dot_general | solution.py:23
  210.0 11.5 %multiply_convert_fusion.1 = bf16[1024,2048]{1,0:T(8,128)(2,1)} fusion(f32[1024]{0:T(1024)S(1)} %mul.66, bf16[1,704,2048]{2,1,0:T(8,128)(2,1)S(1)} %copy-done, f32[1024,704]{0,1:T(8,128)} %fusion.4, bf16[1024,2048]{1,0:T(8,128)(2,1)} %all-gather.6.cloned.1.call-done, bf16[1,2048,704]{1,2,0:T(8,128)(2,1)} %param.21), kind=kOutput, calls=%fused_computation.1 | convolution fusion | flops 5918294016 | bytes 17043456 | tf_op jit(solution)/shard_map/dot_general | solution.py:25
  221.9 31.4 %all-gather.8.cloned.1.call-done = bf16[1024,2048]{1,0:T(8,128)(2,1)} async-done(((bf16[64,2048]{1,0:T(8,128)(2,1)}), bf16[1024,2048]{1,0:T(8,128)(2,1)}) %all-gather.8.cloned.1.call-update) | async-done | bytes 4194320 | tf_op jit(solution)/shard_map/all_gather | solution.py:166
  253.2 7.8 %fusion.2 = f32[1024,704]{0,1:T(8,128)} fusion(bf16[1024,2048]{1,0:T(8,128)(2,1)} %all-gather.8.cloned.1.call-done, bf16[1,2048,704]{1,2,0:T(8,128)(2,1)} %param.22), kind=kOutput, calls=%fused_computation.4 | convolution fusion | flops 2952790016 | bytes 9961472 | tf_op jit(solution)/shard_map/dot_general | solution.py:23
  261.1 11.6 %multiply_convert_fusion = bf16[1024,2048]{1,0:T(8,128)(2,1)} fusion(f32[1024]{0:T(1024)S(1)} %mul.76, bf16[1,704,2048]{2,1,0:T(8,128)(2,1)S(1)} %copy-done, f32[1024,704]{0,1:T(8,128)} %fusion.2, bf16[1024,2048]{1,0:T(8,128)(2,1)} %all-gather.8.cloned.1.call-done, bf16[1,2048,704]{1,2,0:T(8,128)(2,1)} %param.21), kind=kOutput, calls=%fused_computation | convolution fusion | flops 5918294016 | bytes 17043456 | tf_op jit(solution)/shard_map/dot_general | solution.py:25
  272.7 54.1 %reduce-scatter.3.cloned.1.call-done = bf16[64,2048]{1,0:T(8,128)(2,1)} async-done(((bf16[1024,2048]{1,0:T(8,128)(2,1)}), bf16[64,2048]{1,0:T(8,128)(2,1)}) %reduce-scatter.3.cloned.1.call-update) | async-done | bytes 262160 | tf_op jit(solution)/shard_map/reduce_scatter | solution.py:171
  326.8 75.6 %reduce-scatter.5.cloned.1.call-done = bf16[64,2048]{1,0:T(8,128)(2,1)} async-done(((bf16[1024,2048]{1,0:T(8,128)(2,1)}), bf16[64,2048]{1,0:T(8,128)(2,1)}) %reduce-scatter.5.cloned.1.call-update) | async-done | bytes 262160 | tf_op jit(solution)/shard_map/reduce_scatter | solution.py:171
  402.3 1.4 add_convert_fusion
  (46 shorter events, 7.6 us)
Async XLA Ops:
  6.5 203.5 %copy-start = (bf16[1,704,2048]{2,1,0:T(8,128)(2,1)S(1)}, bf16[1,704,2048]{2,1,0:T(8,128)(2,1)}, u32[]{:S(2)}) copy-start(bf16[1,704,2048]{2,1,0:T(8,128)(2,1)} %param.23) | copy-start | bytes 8650756
  6.5 139.1 %all-gather.4.cloned.1.call-start = ((), (), s32[]{:S(2)}) async-start(), calls=%async_computation.5 | async-start | bytes 8650752 | tf_op jit(solution)/shard_map/all_gather | solution.py:142
  7.3 9.8 %copy-start.3 = (bf16[64,2,64]{2,1,0:T(2,128)(2,1)S(1)}, bf16[64,2,64]{2,1,0:T(2,128)(2,1)}, u32[]{:S(2)}) copy-start(bf16[64,2,64]{2,1,0:T(2,128)(2,1)} %param.15) | copy-start | bytes 49156
  10.8 7.1 %slice-start = ((bf16[64,2,16,192]{3,2,1,0:T(8,128)(2,1)}), bf16[64,2,16,128]{3,2,1,0:T(8,128)(2,1)S(1)}, s32[]{:S(2)}) async-start(bf16[64,2,16,192]{3,2,1,0:T(8,128)(2,1)} %reshape.59), calls=%async_computation.10 | async-start | bytes 1048576 | tf_op jit(solution)/shard_map/slice | solution.py:108
  31.1 6.6 %copy-start.4 = (s32[2,1024]{1,0:T(2,128)S(1)}, s32[2,1024]{1,0:T(2,128)}, u32[]{:S(2)}) copy-start(s32[2,1024]{1,0:T(2,128)} %param.18) | copy-start | bytes 24580
  31.1 87.8 %all-to-all-start = ((bf16[16,64,1024]{2,1,0:T(8,128)(2,1)}), bf16[16,64,1024]{2,1,0:T(8,128)(2,1)}, u32[]{:S(2)}, u32[]{:S(2)}) async-start(bf16[16,64,1024]{2,1,0:T(8,128)(2,1)} %copy.26), calls=%async_computation | async-start | bytes 4194304 | tf_op jit(solution)/shard_map/all_to_all | solution.py:116
  37.9 81.0 %copy-start.2 = (s32[1024]{0:T(1024)}, s32[1024]{0:T(1024)S(1)}, u32[]{:S(2)}) copy-start(s32[1024]{0:T(1024)S(1)} %multiply_reduce_fusion.1) | copy-start | bytes 12292
  118.9 15.0 %copy-start.5 = (bf16[2048]{0:T(1024)(128)(2,1)S(1)}, bf16[2048]{0:T(1024)(128)(2,1)}, u32[]{:S(2)}) copy-start(bf16[2048]{0:T(1024)(128)(2,1)} %param.20) | copy-start | bytes 12292
  126.9 18.3 %all-to-all-start.1 = ((bf16[16,64,256]{2,1,0:T(8,128)(2,1)}), bf16[16,64,256]{2,1,0:T(8,128)(2,1)S(1)}, u32[]{:S(2)}, u32[]{:S(2)}) async-start(bf16[16,64,256]{2,1,0:T(8,128)(2,1)} %bitcast.57), calls=%async_computation.1 | async-start | bytes 1048576 | tf_op jit(solution)/shard_map/all_to_all | solution.py:126
  131.6 70.5 %all-gather.6.cloned.1.call-start = ((), (), s32[]{:S(2)}) async-start(), calls=%async_computation.6 | async-start | bytes 4456448 | tf_op jit(solution)/shard_map/all_gather | solution.py:166
  150.6 1.0 copy-start.1
  150.6 2.8 copy-start.6
  150.6 2.8 copy-start.7
  152.6 100.6 %all-gather.8.cloned.1.call-start = ((), (), s32[]{:S(2)}) async-start(), calls=%async_computation.8 | async-start | bytes 4456448 | tf_op jit(solution)/shard_map/all_gather | solution.py:166
  153.3 173.4 %reduce-scatter.3.cloned.1.call-start = ((), (), s32[]{:S(2)}) async-start(), calls=%async_computation.7 | async-start | bytes 4456448 | tf_op jit(solution)/shard_map/reduce_scatter | solution.py:171
  221.5 180.8 %reduce-scatter.5.cloned.1.call-start = ((), (), s32[]{:S(2)}) async-start(), calls=%async_computation.9 | async-start | bytes 4456448 | tf_op jit(solution)/shard_map/reduce_scatter | solution.py:171
Sparse Core Ops, SparseCore 0:
  10.2 104.3 all-gather.3
  152.7 49.3 all-gather.5
  204.3 48.8 all-gather.7
  257.0 69.7 reduce-scatter.2
  330.5 71.8 reduce-scatter.4
